TPU v7x, 128 devices: a whole 4x4x4 slice. The times are simulated.
128 devices in a mesh: tm: 32 (over z, y, core), freq: 4 (over x).
Axes of the slice: x: 4, y: 4, z: 4, core: 2. Of those that a mesh axis runs over, the one named last changes fastest.
Arguments:
- spectrum: bfloat16 [4096, 262144], P('freq', 'tm'), may hold values from 4 to 160
- templates: float32 [4096, 128], P('freq'), may hold values from 0.02 to 2.1
- activations: float32 [128, 262144], P(None, 'tm'), may hold values from 0.06 to 6
- lengths: int32 [512], P('tm'), may hold values from 1 to 512
Outputs:
- new_activations: float32 [128, 262144], P(None, 'tm')
- new_templates: float32 [4096, 128], P('freq')
Inputs may be any that keep to these rules, and one draw needn't show every extreme that they name: Track j holds frame slots j * 512 to (j + 1) * 512 - 1; its first lengths[j] slots are frames, the rest padding whose spectrum is arbitrary.
All inputs are finite; a program needn't handle non-finite values.
Results may differ from a plain program's by a relative error of at most 0.0003.
Values sent between devices are 32-bit elements; how exact they have to be, the bound alone decides.
A program may use at most 128 MiB of HBM per device.

v0:
```python
import functools

import jax
import jax.numpy as jnp
from jax import lax
from jax.experimental import pallas as pl
from jax.experimental.pallas import tpu as pltpu
from jax.sharding import PartitionSpec as P

MESH = pl.DeviceIdType.MESH
TRACK_LEN = 512
UPDATES = 2
AHEAD = 6
SIZES = (4096, 4928, 5184, 5376, 5632, 5824, 6272, 8192)
CHUNKS = (8, 7, 9, 7, 8, 7, 7, 8)
MIB = 1024 * 1024

F32 = jnp.float32
BF16 = jnp.bfloat16
VMEM = pltpu.VMEM


def split(x):
    high = x.astype(BF16)
    low = (x - high.astype(F32)).astype(BF16)
    return high, low


def right_operand(m):
    high, low = split(m)
    top = jnp.concatenate([high, low], axis=1)
    bottom = jnp.concatenate([high, jnp.zeros_like(low)], axis=1)
    return jnp.concatenate([top, bottom], axis=0)


def fine_dot(x, operand):
    high, low = split(x)
    both = jnp.dot(jnp.concatenate([high, low], axis=1), operand, preferred_element_type=F32)
    k = both.shape[1] // 2
    return both[:, :k] + both[:, k:]


def fold_quadrants(m):
    k = m.shape[0] // 2
    return (m[:k, :k] + m[k:, k:]) + (m[:k, k:] + m[k:, :k])


def on_hbm(x):
    return pltpu.with_memory_space_constraint(x, pltpu.HBM)


def send(src, dst, send_sem, recv_sem, device):
    return pltpu.make_async_remote_copy(
        src_ref=src, dst_ref=dst, send_sem=send_sem, recv_sem=recv_sem,
        device_id=device, device_id_type=MESH,
    )


def numerator_kernel(
    ntm, nfreq, steps, spec_hbm, templates_ref, act_hbm, lengths_ref,
    num_ref, act_out_ref, operand_ref, src_ref, branch_ref, spec,
    act, low_ref, gram_ref, grams_ref, count_ref, counts_ref,
    spec_sem, act_sem, gram_send, gram_recv, count_send, count_recv,
):
    t = lax.axis_index("tm")
    r = lax.axis_index("freq")

    barrier = pltpu.get_barrier_semaphore()

    @pl.loop(1, ntm)
    def _(k):
        pl.semaphore_signal(barrier, inc=1, device_id=(lax.rem(t + k, ntm), r), device_id_type=MESH)

    @pl.loop(1, nfreq)
    def _(k):
        pl.semaphore_signal(barrier, inc=1, device_id=(t, lax.rem(r + k, nfreq)), device_id_type=MESH)

    def columns(i):
        return pl.ds(pl.multiple_of(i * TRACK_LEN, TRACK_LEN), TRACK_LEN)

    def act_copy(i):
        return pltpu.make_async_copy(act_hbm.at[:, columns(i)], act.at[i], act_sem.at[i])

    def spec_copy(i):
        return pltpu.make_async_copy(spec_hbm.at[:, columns(i)], spec.at[i], spec_sem.at[i])

    @pl.loop(0, steps)
    def _(i):
        act_copy(i).start()

    @pl.loop(0, AHEAD)
    def _(i):
        spec_copy(i).start()

    index = lax.broadcasted_iota(jnp.int32, (8, 128), 0) * 128 + lax.broadcasted_iota(jnp.int32, (8, 128), 1)
    table = index
    total = jnp.int32(0)
    per_track = TRACK_LEN // 8
    for j in range(steps):
        tiles = (lengths_ref[j] + 7) // 8
        total = total + tiles
        table = table + jnp.where(index >= total, per_track - tiles, 0)
    src_ref[...] = jnp.minimum(table, steps * per_track - 1)
    count_ref[...] = jnp.full((8, 128), total.astype(F32))

    turned = templates_ref[...].T
    high_t, low_t = split(turned)
    low_ref[...] = high_t
    high, low = split(templates_ref[...])
    products = jnp.dot(
        jnp.concatenate([high_t, low_t], axis=0),
        jnp.concatenate([high, low], axis=1),
        preferred_element_type=F32,
    )
    gram_ref[...] = fold_quadrants(products)

    @pl.loop(0, steps)
    def _(i):
        act_copy(i).wait()
        at = pl.ds(pl.multiple_of(i * per_track, per_track), per_track)
        act_out_ref[at] = act[i].T.reshape(per_track, 8, -1)

    pl.semaphore_wait(barrier, ntm + nfreq - 2)

    def gram_copy(k):
        return send(gram_ref, grams_ref.at[k - 1], gram_send.at[k - 1], gram_recv.at[k - 1], (t, lax.rem(r + k, nfreq)))

    for k in range(1, nfreq):
        gram_copy(k).start()
    for k in range(1, ntm):
        send(count_ref, counts_ref.at[k - 1], count_send, count_recv, (lax.rem(t + k, ntm), r)).start()

    @pl.loop(0, steps)
    def _(i):
        spec_copy(i).wait()

        @pl.when(i + AHEAD < steps)
        def _():
            spec_copy(i + AHEAD).start()

        num = jnp.dot(low_ref[...], spec[i], preferred_element_type=F32)
        at = pl.ds(pl.multiple_of(i * per_track, per_track), per_track)
        num_ref[at] = num.T.reshape(per_track, 8, -1)

    everyone = send(counts_ref, counts_ref, count_send, count_recv, (lax.rem(t + 1, ntm), r))
    everyone.wait_send()
    everyone.wait_recv()
    most = count_ref[...]
    for k in range(ntm - 1):
        most = jnp.maximum(most, counts_ref[k])
    needed = jnp.max(most) * 8.0
    branch = jnp.int32(0)
    for size in SIZES[:-1]:
        branch = branch + (needed > size).astype(jnp.int32)
    branch_ref[0] = branch
    gram = gram_ref[...]
    for k in range(1, nfreq):
        gram_copy(k).wait_send()
        gram_copy(k).wait_recv()
        gram = gram + grams_ref[k - 1]
    operand_ref[...] = right_operand(gram)


def numerator_call(mesh, spectrum, templates, activations, lengths):
    ntm, nfreq = mesh.shape["tm"], mesh.shape["freq"]
    bins, frames = spectrum.shape
    k = templates.shape[1]
    steps = frames // TRACK_LEN
    whole = pl.BlockSpec(memory_space=VMEM)
    scalars = pl.BlockSpec(memory_space=pltpu.SMEM)
    far = pl.BlockSpec(memory_space=pltpu.HBM)
    return pl.pallas_call(
        functools.partial(numerator_kernel, ntm, nfreq, steps),
        out_shape=(
            VMEM((frames // 8, 8, k), F32),
            VMEM((frames // 8, 8, k), F32),
            jax.ShapeDtypeStruct((2 * k, 2 * k), BF16),
            jax.ShapeDtypeStruct((8, 128), jnp.int32),
            jax.ShapeDtypeStruct((1,), jnp.int32),
            VMEM((steps, bins, TRACK_LEN), BF16),
        ),
        in_specs=[far, whole, far, scalars],
        out_specs=(whole, whole, whole, whole, scalars, whole),
        scratch_shapes=[
            VMEM((steps, k, TRACK_LEN), F32),
            VMEM((k, bins), BF16),
            VMEM((k, k), F32),
            VMEM((nfreq - 1, k, k), F32),
            VMEM((8, 128), F32),
            VMEM((ntm - 1, 8, 128), F32),
            pltpu.SemaphoreType.DMA((steps,)),
            pltpu.SemaphoreType.DMA((steps,)),
            pltpu.SemaphoreType.DMA((nfreq - 1,)),
            pltpu.SemaphoreType.DMA((nfreq - 1,)),
            pltpu.SemaphoreType.DMA,
            pltpu.SemaphoreType.DMA,
        ],
        compiler_params=pltpu.CompilerParams(
            collective_id=0, has_side_effects=True, vmem_limit_bytes=8 * MIB,
        ),
        name="numerator",
    )(on_hbm(spectrum), templates, on_hbm(activations), lengths)


def refine_kernel(
    size, chunks, src_ref, num_ref, act_ref, operand_ref, out_ref,
    comp, own, first, direct, second, send_sem, first_sem, direct_sem, second_sem, near_sem, far_sem,
):
    t = lax.axis_index("tm")
    r = lax.axis_index("freq")
    shard, half = size // 4, size // 8
    cw = half // chunks
    right, left, opposite = lax.rem(r + 1, 4), lax.rem(r + 3, 4), lax.rem(r + 2, 4)
    near = ((t, right), (t, left))

    barrier = pltpu.get_barrier_semaphore()
    for device in near:
        pl.semaphore_signal(barrier, inc=1, device_id=device, device_id_type=MESH)

    def rows(base, h, c):
        return pl.ds(pl.multiple_of(base * shard + h * half + c * cw, 8), cw)

    def part(c):
        return pl.ds(pl.multiple_of(c * cw, 8), cw)

    def gather(base, h, c, table, into, offset):
        start = base * shard + h * half + c * cw
        for i in range(cw // 8):
            tile = start // 8 + i
            source = src_ref[tile // 128, tile % 128]
            into[pl.ds(pl.multiple_of(start - offset + 8 * i, 8), 8), :] = table[source]

    def first_copy(way, c):
        return send(comp.at[rows(opposite, way, c)], first.at[way, part(c)], send_sem.at[way], first_sem.at[way, c], near[way])

    def direct_copy(way, c):
        return send(comp.at[rows((right, left)[way], 1 - way, c)], direct.at[way, part(c)], send_sem.at[2 + way], direct_sem.at[way, c], near[way])

    def second_copy(way, c):
        return send(first.at[way, part(c)], second.at[way, part(c)], send_sem.at[4 + way], second_sem.at[way, c], near[way])

    def near_copy(way, h, c):
        return send(out_ref.at[rows(r, h, c)], out_ref.at[rows(r, h, c)], send_sem.at[6 + 2 * way + h], near_sem.at[way, h, c], near[way])

    def near_arrival(way, h, c):
        owner = (left, right)[way]
        return send(out_ref.at[rows(owner, h, c)], out_ref.at[rows(owner, h, c)], send_sem.at[6 + 2 * way + h], near_sem.at[way, h, c], near[way])

    def far_copy(way, c):
        owner = (left, right)[way]
        return send(out_ref.at[rows(owner, way, c)], out_ref.at[rows(owner, way, c)], send_sem.at[10 + way], far_sem.at[way, c], near[way])

    def far_arrival(way, c):
        return send(out_ref.at[rows(opposite, way, c)], out_ref.at[rows(opposite, way, c)], send_sem.at[10 + way], far_sem.at[way, c], near[way])

    for way in range(2):
        gather(opposite, way, 0, num_ref, comp, 0)
    pl.semaphore_wait(barrier, 2)
    for way in range(2):
        first_copy(way, 0).start()

    @pl.loop(1, chunks)
    def _(c):
        for way in range(2):
            gather(opposite, way, c, num_ref, comp, 0)
            first_copy(way, c).start()

    @pl.loop(0, chunks)
    def _(c):
        for way in range(2):
            gather((right, left)[way], 1 - way, c, num_ref, comp, 0)
            direct_copy(way, c).start()

    @pl.loop(0, chunks)
    def _(c):
        for way in range(2):
            gather((right, left)[way], way, c, num_ref, comp, 0)
            gather(r, way, c, num_ref, comp, 0)
            gather(r, way, c, act_ref, own, r * shard)

    @pl.loop(0, chunks)
    def _(c):
        for way in range(2):
            first_copy(way, c).wait_recv()
            first[way, part(c), :] = first[way, part(c), :] + comp[rows((right, left)[way], way, c), :]
            second_copy(way, c).start()

    @pl.loop(0, chunks)
    def _(c):
        for h in range(2):
            second_copy(h, c).wait_recv()
            direct_copy(1 - h, c).wait_recv()
            numerator = comp[rows(r, h, c), :] + second[h, part(c), :] + direct[1 - h, part(c), :]
            current = own[pl.ds(pl.multiple_of(h * half + c * cw, 8), cw), :]
            for _ in range(UPDATES):
                current = current * numerator / fine_dot(current, operand_ref[...])
            out_ref[rows(r, h, c), :] = current
            for way in range(2):
                near_copy(way, h, c).start()

    @pl.loop(0, chunks)
    def _(c):
        for way in range(2):
            near_arrival(way, way, c).wait_recv()
            far_copy(way, c).start()

    @pl.loop(0, chunks)
    def _(c):
        for way in range(2):
            near_arrival(way, 1 - way, c).wait_recv()
            far_arrival(way, c).wait_recv()

    for i in range(12):
        whole = first.at[0]
        send(whole, whole, send_sem.at[i], first_sem.at[0, 0], near[0]).wait_send()


def refine_call(size, index, src, num, act, operand):
    frames, k = num.shape[0] * 8, num.shape[2]
    shard, half = size // 4, size // 8
    chunks = CHUNKS[index]
    whole = pl.BlockSpec(memory_space=VMEM)
    return pl.pallas_call(
        functools.partial(refine_kernel, size, chunks),
        out_shape=VMEM((frames, k), F32),
        in_specs=[pl.BlockSpec(memory_space=pltpu.SMEM), whole, whole, whole],
        out_specs=whole,
        scratch_shapes=[
            VMEM((size, k), F32),
            VMEM((shard, k), F32),
            VMEM((2, half, k), F32),
            VMEM((2, half, k), F32),
            VMEM((2, half, k), F32),
            pltpu.SemaphoreType.DMA((12,)),
            pltpu.SemaphoreType.DMA((2, chunks)),
            pltpu.SemaphoreType.DMA((2, chunks)),
            pltpu.SemaphoreType.DMA((2, chunks)),
            pltpu.SemaphoreType.DMA((2, 2, chunks)),
            pltpu.SemaphoreType.DMA((2, chunks)),
        ],
        compiler_params=pltpu.CompilerParams(
            collective_id=1 + index, has_side_effects=True, vmem_limit_bytes=12 * MIB,
        ),
        name=f"refine_{size}",
    )(src, num, act, operand)


def template_kernel(
    steps, lengths_ref, act_ref, spec, templates_ref, placed_ref, out_ref,
    high_ref, denominator_ref, expanded, gram_ref, stage, pair, den_pair, land, den_land,
    stage_send, pair_recv, den_pair_send, den_pair_recv, land_send, land_recv, den_send, den_recv,
    out_send, out_recv, last_send, last_recv,
):
    t = lax.axis_index("tm")
    r = lax.axis_index("freq")
    core = lax.rem(t, 2)
    y = lax.rem(t // 2, 4)
    z = t // 8
    bins = templates_ref.shape[0]
    half = bins // 2
    block = bins // 8
    count = block // 4
    partner = (t + 1 - 2 * core, r)
    def there(q):
        return lax.rem(z + q, 4)

    def device(q, s):
        return ((there(q) * 4 + lax.rem(y + s, 4)) * 2 + core, r)

    def each_peer(do):
        @pl.loop(1, 16)
        def _(k):
            do(k // 4, lax.rem(k, 4))

    barrier = pltpu.get_barrier_semaphore()
    pl.semaphore_signal(barrier, inc=1, device_id=partner, device_id_type=MESH)
    each_peer(lambda q, s: pl.semaphore_signal(barrier, inc=1, device_id=device(q, s), device_id_type=MESH))

    gram_ref[...] = jnp.zeros_like(gram_ref)
    position = lax.broadcasted_iota(jnp.int32, (8, templates_ref.shape[1]), 0)

    def place(i, start):
        length = lengths_ref[i]
        for j in range(TRACK_LEN // 8):
            expanded[8 * j : 8 * j + 8, :] = jnp.where(position + 8 * j < length, act_ref[start + j], 0.0)
        x = expanded[...]
        turned = x.T
        placed_ref[:, pl.ds(pl.multiple_of(i * TRACK_LEN, TRACK_LEN), TRACK_LEN)] = turned
        high, low = split(x)
        high_ref[i] = high
        high_t, low_t = split(turned)
        gram_ref[...] += jnp.dot(
            jnp.concatenate([high_t, low_t], axis=0),
            jnp.concatenate([high, low], axis=1),
            preferred_element_type=F32,
        )
        return start + (length + 7) // 8

    lax.fori_loop(0, steps, place, jnp.int32(0))
    denominator_ref[...] = fine_dot(templates_ref[...], right_operand(fold_quadrants(gram_ref[...])))
    pl.semaphore_wait(barrier, 16)

    theirs = pl.ds(pl.multiple_of((1 - core) * half, half), half)
    mine = pl.ds(pl.multiple_of(core * half, half), half)
    den_copy = send(denominator_ref.at[theirs], den_pair, den_pair_send, den_pair_recv, partner)
    den_copy.start()

    def pair_copy(q):
        return send(stage.at[0, q], pair.at[q], stage_send.at[q], pair_recv.at[q], partner)

    def piece(s):
        return pl.ds(pl.multiple_of(lax.rem(y + s, 4) * count, count), count)

    def den_piece(q, s):
        at = pl.ds(pl.multiple_of(there(q) * block + lax.rem(y + s, 4) * count, count), count)
        return send(den_pair.at[at], den_land.at[q * 4 + s - 1], den_send, den_recv, device(q, s))

    def cross_piece(q, s):
        return send(stage.at[1, q, piece(s)], land.at[q * 4 + s - 1], land_send, land_recv, device(q, s))

    @pl.loop(0, 8)
    def _(n):
        own_side = n // 4
        q = lax.rem(n + 1, 4)
        side = lax.rem(core + 1 + own_side, 2)
        rows = pl.ds(pl.multiple_of((side * 4 + there(q)) * block, block), block)
        total = jnp.dot(spec[0, rows, :], high_ref[0], preferred_element_type=F32)
        for i in range(1, steps):
            total = total + jnp.dot(spec[i, rows, :], high_ref[i], preferred_element_type=F32)
        stage[own_side, q] = total

        @pl.when(n < 4)
        def _():
            pair_copy(q).start()

        @pl.when(n == 1)
        def _():
            den_copy.wait()
            den_pair[...] = den_pair[...] + denominator_ref[mine, :]
            each_peer(lambda q, s: den_piece(q, s).start())

        @pl.when(n >= 4)
        def _():
            pair_copy(q).wait_recv()
            stage[1, q] = stage[1, q] + pair[q]
            for s in (1, 2, 3):
                cross_piece(q, s).start()

            @pl.when(q > 0)
            def _():
                cross_piece(q, 0).start()

    den_all = send(den_land, den_land, den_send, den_recv, partner)
    cross_all = send(land, land, land_send, land_recv, partner)
    den_all.wait_recv()
    offset = z * block + y * count
    denominator = den_pair[pl.ds(pl.multiple_of(offset, count), count), :]
    for k in range(15):
        denominator = denominator + den_land[k]
    cross_all.wait_recv()
    cross = stage[1, 0, piece(0), :]
    for k in range(15):
        cross = cross + land[k]
    own = pl.ds(pl.multiple_of(core * half + offset, count), count)
    out_ref[own, :] = templates_ref[own, :] * cross / denominator

    each_peer(lambda q, s: send(out_ref.at[own], out_ref.at[own], out_send, out_recv, device(q, s)).start())

    others = out_ref.at[pl.ds(0, 15 * count)]
    gathered = send(others, others, out_send, out_recv, partner)
    gathered.wait_recv()
    last = send(out_ref.at[mine], out_ref.at[mine], last_send, last_recv, partner)
    last.start()
    last.wait_recv()
    for q in range(4):
        pair_copy(q).wait_send()
    for copy in (den_all, cross_all, gathered, last):
        copy.wait_send()


def template_call(index, lengths, act, spectrum, templates):
    bins, k = templates.shape
    steps = spectrum.shape[0]
    half, block, count = bins // 2, bins // 8, bins // 32
    whole = pl.BlockSpec(memory_space=VMEM)
    one = pltpu.SemaphoreType.DMA
    return pl.pallas_call(
        functools.partial(template_kernel, steps),
        out_shape=(VMEM((k, steps * TRACK_LEN), F32), jax.ShapeDtypeStruct((bins, k), F32)),
        in_specs=[pl.BlockSpec(memory_space=pltpu.SMEM)] + [whole] * 3,
        out_specs=(whole, whole),
        scratch_shapes=[
            VMEM((steps, TRACK_LEN, k), BF16),
            VMEM((bins, k), F32),
            VMEM((TRACK_LEN, k), F32),
            VMEM((2 * k, 2 * k), F32),
            VMEM((2, 4, block, k), F32),
            VMEM((4, block, k), F32),
            VMEM((half, k), F32),
            VMEM((15, count, k), F32),
            VMEM((15, count, k), F32),
            one((4,)), one((4,)), one, one, one, one, one, one, one, one, one, one,
        ],
        compiler_params=pltpu.CompilerParams(
            collective_id=1 + len(SIZES) + index, has_side_effects=True, vmem_limit_bytes=8 * MIB
        ),
        name=f"templates_{index}",
    )(lengths, act, spectrum, templates)


def store_kernel(placed_ref, out_hbm, sem):
    k = placed_ref.shape[0]
    parts = 8
    copies = []
    for i in range(parts):
        rows = pl.ds(i * (k // parts), k // parts)
        copies.append(pltpu.make_async_copy(placed_ref.at[rows], out_hbm.at[rows], sem.at[i]))
    for copy in copies:
        copy.start()
    for copy in copies:
        copy.wait()


def store_call(placed):
    return pl.pallas_call(
        store_kernel,
        out_shape=jax.ShapeDtypeStruct(placed.shape, placed.dtype),
        in_specs=[pl.BlockSpec(memory_space=VMEM)],
        out_specs=pl.BlockSpec(memory_space=pltpu.HBM),
        scratch_shapes=[pltpu.SemaphoreType.DMA((8,))],
        compiler_params=pltpu.CompilerParams(vmem_limit_bytes=5 * MIB),
        name="store",
    )(placed)


def rest(size, index, src, num, act, operand, lengths, spectrum, templates):
    current = refine_call(size, index, src, num, act, operand)
    current = current.reshape(current.shape[0] // 8, 8, -1)
    placed, new_templates = template_call(index, lengths, current, spectrum, templates)
    return store_call(placed), new_templates


def body(mesh, spectrum, templates, activations, lengths):
    num, act, operand, src, branch, near_spectrum = numerator_call(mesh, spectrum, templates, activations, lengths)
    branches = [functools.partial(rest, size, i) for i, size in enumerate(SIZES)]
    return lax.switch(branch[0], branches, src, num, act, operand, lengths, near_spectrum, templates)


def solution(mesh):
    return jax.shard_map(
        functools.partial(body, mesh),
        mesh=mesh,
        in_specs=(P("freq", "tm"), P("freq", None), P(None, "tm"), P("tm")),
        out_specs=(P(None, "tm"), P("freq", None)),
        check_vma=False,
    )
```

profile of v0, /device:TPU:1, one launch (start us, length us, event | category | flops | bytes accessed | tf_op | source)
XLA Modules:
  0.0 97.1 jit_solution(3591120872985688175)
XLA Ops:
  0.6 0.0 copy-start.1
  0.6 0.0 copy-start
  0.7 16.9 %numerator.1 = (f32[1024,8,128]{2,1,0:T(8,128)S(1)}, f32[1024,8,128]{2,1,0:T(8,128)S(1)}, bf16[256,256]{1,0:T(8,128)(2,1)S(1)}, s32[8,128]{1,0:T(8,128)S(1)}, s3...) custom-call(bf16[1024,8192]{1,0:T(8,128)(2,1)} %spec_hbm.1, f32[1024,128]{1,0:T(8,128)} %templates_ref.1, f32[128,8192]{1,0:T(8,128)} %act_hbm.1, ...), custom_call_target="tpu_custom_call" | custom-call | tf_op jit(solution)/shard_map/numerator/pallas_call | solution.py:172
  18.3 0.0 copy-done.1
  18.3 0.0 copy-done
  18.3 78.0 %conditional.1 = (f32[1024,128]{1,0:T(8,128)S(1)}, f32[128,8192]{1,0:T(8,128)}) conditional(s32[]{:T(128)} %bitcast.8, (s32[8,128]{1,0:T(8,128)S(1)}, f32[1024,8,128]{2,1,0:T(8,128)S(1)}, f32[1024,8,128]{2,1,0:T(8,128)S(1)}, bf16[256,256]{1,0:T(8,128)(2,1)S(1)}, s32[16]{0:T(128)S(1)}, ...), branch_computations={%region_0.0_spmd, %region_1.0_spmd, %region_2.0_spmd, %region_3.0_... | conditional | bytes 16 | solution.py:546
  18.5 49.3 %refine_5376.1 = f32[8192,128]{1,0:T(8,128)S(1)} custom-call(s32[8,128]{1,0:T(8,128)S(1)} %get-tuple-element.140.src_ref, f32[1024,8,128]{2,1,0:T(8,128)S(1)} %get-tuple-element.141.num_ref, f32[1024,8,128]{2,1,0:T(8,128)S(1)} %get-tuple-element.142.act_ref, bf16[256,256]{1,0:T(8,128)(2,1)S(1)} %get-tuple-element.143.operand_ref), custom_call_target="tpu_custom_call" | custom-call | tf_op jit(solution)/shard_map/cond/branch_3_fun/refine_5376/pallas_call | solution.py:323
  67.9 25.8 %templates_3.1 = (f32[128,8192]{1,0:T(8,128)S(1)}, f32[1024,128]{1,0:T(8,128)S(1)}) custom-call(s32[16]{0:T(128)S(1)} %get-tuple-element.139.lengths_ref, f32[1024,8,128]{2,1,0:T(8,128)S(1)} %bitcast.12, bf16[16,1024,512]{2,1,0:T(8,128)(2,1)S(1)} %get-tuple-element.144.spec, f32[1024,128]{1,0:T(8,128)S(1)} %get-tuple-element.145.templates_ref), custom_call_target="tpu_custom_call" | custom-call | tf_op jit(solution)/shard_map/cond/branch_3_fun/templates_3/pallas_call | solution.py:487
  93.7 2.1 %store.11 = f32[128,8192]{1,0:T(8,128)} custom-call(f32[128,8192]{1,0:T(8,128)S(1)} %get-tuple-element.146.placed_ref), custom_call_target="tpu_custom_call" | custom-call | tf_op jit(solution)/shard_map/cond/branch_3_fun/store/pallas_call | solution.py:525
  96.3 0.8 copy.31
Async XLA Ops:
  0.6 17.7 %copy-start.1 = (s32[16]{0:T(128)S(1)}, s32[16]{0:T(128)}, u32[]{:S(2)}) copy-start(s32[16]{0:T(128)} %lengths_ref.1) | copy-start | bytes 196
  0.6 17.7 %copy-start = (f32[1024,128]{1,0:T(8,128)S(1)}, f32[1024,128]{1,0:T(8,128)}, u32[]{:S(2)}) copy-start(f32[1024,128]{1,0:T(8,128)} %templates_ref.1) | copy-start | bytes 1572868
where the time goes:
time: 97.2 us; the launch traced here: 97.1 us
  Pallas kernels  94.2 us (97%)
  between operations  1.37 us (1%)
    pallas_call x1, Pallas kernels, refine_call(): pl.pallas_call(functools.partial(refine_kernel, size, chunks), out_shape=...  49.3 us
    pallas_call x1, Pallas kernels, template_call(): pl.pallas_call(functools.partial(template_kernel, steps), out_shape=(VMEM...  25.8 us
    pallas_call x1, Pallas kernels, numerator_call(): pl.pallas_call(functools.partial(numerator_kernel, ntm, nfreq, steps), ou...  16.9 us
    pallas_call x1, Pallas kernels, store_call(): pl.pallas_call(store_kernel, out_shape=jax.ShapeDtypeStruct(placed.shape,...  2.07 us

commit v1 on v0

--- a/solution.py
+++ b/solution.py
@@ -57,14 +57,35 @@
 
 
 def numerator_kernel(
-    ntm, nfreq, steps, spec_hbm, templates_ref, act_hbm, lengths_ref,
+    ntm, nfreq, steps, spec_hbm, templates_hbm, act_hbm, lengths_ref,
     num_ref, act_out_ref, operand_ref, src_ref, branch_ref, spec,
-    act, low_ref, gram_ref, grams_ref, count_ref, counts_ref,
-    spec_sem, act_sem, gram_send, gram_recv, count_send, count_recv,
+    act, templates_ref, low_ref, gram_ref, grams_ref, count_ref, counts_ref,
+    templates_sem, spec_sem, act_sem, gram_send, gram_recv, count_send, count_recv,
 ):
     t = lax.axis_index("tm")
     r = lax.axis_index("freq")
 
+    def columns(i):
+        return pl.ds(pl.multiple_of(i * TRACK_LEN, TRACK_LEN), TRACK_LEN)
+
+    def act_copy(i):
+        return pltpu.make_async_copy(act_hbm.at[:, columns(i)], act.at[i], act_sem.at[i])
+
+    def spec_copy(i):
+        return pltpu.make_async_copy(spec_hbm.at[:, columns(i)], spec.at[i], spec_sem.at[i])
+
+    templates_copy = pltpu.make_async_copy(templates_hbm, templates_ref, templates_sem)
+    templates_copy.start()
+
+    @pl.loop(0, AHEAD)
+    def _(i):
+        act_copy(i).start()
+        spec_copy(i).start()
+
+    @pl.loop(AHEAD, steps)
+    def _(i):
+        act_copy(i).start()
+
     barrier = pltpu.get_barrier_semaphore()
 
     @pl.loop(1, ntm)
@@ -74,23 +95,6 @@
     @pl.loop(1, nfreq)
     def _(k):
         pl.semaphore_signal(barrier, inc=1, device_id=(t, lax.rem(r + k, nfreq)), device_id_type=MESH)
-
-    def columns(i):
-        return pl.ds(pl.multiple_of(i * TRACK_LEN, TRACK_LEN), TRACK_LEN)
-
-    def act_copy(i):
-        return pltpu.make_async_copy(act_hbm.at[:, columns(i)], act.at[i], act_sem.at[i])
-
-    def spec_copy(i):
-        return pltpu.make_async_copy(spec_hbm.at[:, columns(i)], spec.at[i], spec_sem.at[i])
-
-    @pl.loop(0, steps)
-    def _(i):
-        act_copy(i).start()
-
-    @pl.loop(0, AHEAD)
-    def _(i):
-        spec_copy(i).start()
 
     index = lax.broadcasted_iota(jnp.int32, (8, 128), 0) * 128 + lax.broadcasted_iota(jnp.int32, (8, 128), 1)
     table = index
@@ -103,6 +107,7 @@
     src_ref[...] = jnp.minimum(table, steps * per_track - 1)
     count_ref[...] = jnp.full((8, 128), total.astype(F32))
 
+    templates_copy.wait()
     turned = templates_ref[...].T
     high_t, low_t = split(turned)
     low_ref[...] = high_t
@@ -114,21 +119,8 @@
     )
     gram_ref[...] = fold_quadrants(products)
 
-    @pl.loop(0, steps)
-    def _(i):
-        act_copy(i).wait()
-        at = pl.ds(pl.multiple_of(i * per_track, per_track), per_track)
-        act_out_ref[at] = act[i].T.reshape(per_track, 8, -1)
-
-    pl.semaphore_wait(barrier, ntm + nfreq - 2)
-
     def gram_copy(k):
         return send(gram_ref, grams_ref.at[k - 1], gram_send.at[k - 1], gram_recv.at[k - 1], (t, lax.rem(r + k, nfreq)))
-
-    for k in range(1, nfreq):
-        gram_copy(k).start()
-    for k in range(1, ntm):
-        send(count_ref, counts_ref.at[k - 1], count_send, count_recv, (lax.rem(t + k, ntm), r)).start()
 
     @pl.loop(0, steps)
     def _(i):
@@ -138,9 +130,21 @@
         def _():
             spec_copy(i + AHEAD).start()
 
+        act_copy(i).wait()
         num = jnp.dot(low_ref[...], spec[i], preferred_element_type=F32)
         at = pl.ds(pl.multiple_of(i * per_track, per_track), per_track)
         num_ref[at] = num.T.reshape(per_track, 8, -1)
+        act_out_ref[at] = act[i].T.reshape(per_track, 8, -1)
+
+        @pl.when(i == 3)
+        def _():
+            pl.semaphore_wait(barrier, ntm + nfreq - 2)
+            for k in range(1, nfreq):
+                gram_copy(k).start()
+
+            @pl.loop(1, ntm)
+            def _(k):
+                send(count_ref, counts_ref.at[k - 1], count_send, count_recv, (lax.rem(t + k, ntm), r)).start()
 
     everyone = send(counts_ref, counts_ref, count_send, count_recv, (lax.rem(t + 1, ntm), r))
     everyone.wait_send()
@@ -179,15 +183,17 @@
             jax.ShapeDtypeStruct((1,), jnp.int32),
             VMEM((steps, bins, TRACK_LEN), BF16),
         ),
-        in_specs=[far, whole, far, scalars],
+        in_specs=[far, far, far, scalars],
         out_specs=(whole, whole, whole, whole, scalars, whole),
         scratch_shapes=[
             VMEM((steps, k, TRACK_LEN), F32),
+            VMEM((bins, k), F32),
             VMEM((k, bins), BF16),
             VMEM((k, k), F32),
             VMEM((nfreq - 1, k, k), F32),
             VMEM((8, 128), F32),
             VMEM((ntm - 1, 8, 128), F32),
+            pltpu.SemaphoreType.DMA,
             pltpu.SemaphoreType.DMA((steps,)),
             pltpu.SemaphoreType.DMA((steps,)),
             pltpu.SemaphoreType.DMA((nfreq - 1,)),
@@ -199,7 +205,7 @@
             collective_id=0, has_side_effects=True, vmem_limit_bytes=8 * MIB,
         ),
         name="numerator",
-    )(on_hbm(spectrum), templates, on_hbm(activations), lengths)
+    )(on_hbm(spectrum), on_hbm(templates), on_hbm(activations), lengths)
 
 
 def refine_kernel(

time: 97.2 us -> 96.3 us (level); the launches traced: 97.1 us -> 94.5 us
  Pallas kernels: 94.2 us -> 91.5 us
    pallas_call x1, Pallas kernels: 49.3 us -> 47.3 us  [refine_call(): pl.pallas_call(functools.partial(refine_kernel, size, chunks), out_shape=...]
where the time goes in v1:
time: 96.3 us; the launch traced here: 94.5 us
  Pallas kernels  91.5 us (95%)
  between operations  1.37 us (1%)
    pallas_call x1, Pallas kernels, refine_call(): pl.pallas_call(functools.partial(refine_kernel, size, chunks), out_shape=...  47.3 us
    pallas_call x1, Pallas kernels, template_call(): pl.pallas_call(functools.partial(template_kernel, steps), out_shape=(VMEM...  26.2 us
    pallas_call x1, Pallas kernels, numerator_call(): pl.pallas_call(functools.partial(numerator_kernel, ntm, nfreq, steps), ou...  16 us
    pallas_call x1, Pallas kernels, store_call(): pl.pallas_call(store_kernel, out_shape=jax.ShapeDtypeStruct(placed.shape,...  2.07 us

profile of v1, /device:TPU:1, one launch (start us, length us, event | category | flops | bytes accessed | tf_op | source)
XLA Modules:
  0.0 94.5 jit_solution(6054475743083077783)
XLA Ops:
  0.6 0.0 copy-start.1
  0.6 0.0 copy-start
  0.7 16.0 %numerator.1 = (f32[1024,8,128]{2,1,0:T(8,128)S(1)}, f32[1024,8,128]{2,1,0:T(8,128)S(1)}, bf16[256,256]{1,0:T(8,128)(2,1)S(1)}, s32[8,128]{1,0:T(8,128)S(1)}, s3...) custom-call(bf16[1024,8192]{1,0:T(8,128)(2,1)} %spec_hbm.1, f32[1024,128]{1,0:T(8,128)} %templates_hbm.1, f32[128,8192]{1,0:T(8,128)} %act_hbm.1, ...), custom_call_target="tpu_custom_call" | custom-call | tf_op jit(solution)/shard_map/numerator/pallas_call | solution.py:176
  17.4 0.0 copy-done.1
  17.4 0.0 copy-done
  17.4 76.3 %conditional.1 = (f32[1024,128]{1,0:T(8,128)S(1)}, f32[128,8192]{1,0:T(8,128)}) conditional(s32[]{:T(128)} %bitcast.8, (s32[8,128]{1,0:T(8,128)S(1)}, f32[1024,8,128]{2,1,0:T(8,128)S(1)}, f32[1024,8,128]{2,1,0:T(8,128)S(1)}, bf16[256,256]{1,0:T(8,128)(2,1)S(1)}, s32[16]{0:T(128)S(1)}, ...), branch_computations={%region_0.0_spmd, %region_1.0_spmd, %region_2.0_spmd, %region_3.0_... | conditional | bytes 16 | solution.py:552
  17.4 47.3 %refine_5184.1 = f32[8192,128]{1,0:T(8,128)S(1)} custom-call(s32[8,128]{1,0:T(8,128)S(1)} %get-tuple-element.131.src_ref, f32[1024,8,128]{2,1,0:T(8,128)S(1)} %get-tuple-element.132.num_ref, f32[1024,8,128]{2,1,0:T(8,128)S(1)} %get-tuple-element.133.act_ref, bf16[256,256]{1,0:T(8,128)(2,1)S(1)} %get-tuple-element.134.operand_ref), custom_call_target="tpu_custom_call" | custom-call | tf_op jit(solution)/shard_map/cond/branch_2_fun/refine_5184/pallas_call | solution.py:329
  64.7 26.2 %templates_2.1 = (f32[128,8192]{1,0:T(8,128)S(1)}, f32[1024,128]{1,0:T(8,128)S(1)}) custom-call(s32[16]{0:T(128)S(1)} %get-tuple-element.130.lengths_ref, f32[1024,8,128]{2,1,0:T(8,128)S(1)} %bitcast.11, bf16[16,1024,512]{2,1,0:T(8,128)(2,1)S(1)} %get-tuple-element.135.spec, f32[1024,128]{1,0:T(8,128)S(1)} %get-tuple-element.136.templates_ref), custom_call_target="tpu_custom_call" | custom-call | tf_op jit(solution)/shard_map/cond/branch_2_fun/templates_2/pallas_call | solution.py:493
  90.9 2.1 %store.10 = f32[128,8192]{1,0:T(8,128)} custom-call(f32[128,8192]{1,0:T(8,128)S(1)} %get-tuple-element.137.placed_ref), custom_call_target="tpu_custom_call" | custom-call | tf_op jit(solution)/shard_map/cond/branch_2_fun/store/pallas_call | solution.py:531
  93.7 0.8 copy.31
Async XLA Ops:
  0.6 16.7 %copy-start.1 = (s32[16]{0:T(128)S(1)}, s32[16]{0:T(128)}, u32[]{:S(2)}) copy-start(s32[16]{0:T(128)} %lengths_ref.1) | copy-start | bytes 196
  0.6 16.7 %copy-start = (f32[1024,128]{1,0:T(8,128)S(1)}, f32[1024,128]{1,0:T(8,128)}, u32[]{:S(2)}) copy-start(f32[1024,128]{1,0:T(8,128)} %templates_hbm.1) | copy-start | bytes 1572868
